TPU v7x, 32 devices: a whole 2x2x4 slice. The times are simulated.
32 devices in a mesh: dp: 8 (over y, x, core), tensor: 4 (over z).
Axes of the slice: x: 2, y: 2, z: 4, core: 2. Of those that a mesh axis runs over, the one named last changes fastest.
Arguments:
- inputs: bfloat16 [584, 16, 1024], P('tensor', 'dp'), may hold values from -6 to 6
- valid_mask: int32 [16, 584], P('dp'), may hold values from 0 to 1, as said below
- cotangent: bfloat16 [584, 16, 1024], P('tensor', 'dp'), may hold values from -60 to 60
- ln_gain: bfloat16 [2, 1024], P(None, 'dp'), may hold values from 0.25 to 1.75
- d_bias: bfloat16 [4, 1024], P(None, 'dp'), may hold values from -3 to 3
- w_qkv: bfloat16 [1024, 3, 1024], P('dp', None, 'tensor'), may hold values from -0.1875 to 0.1875
- b_qv: bfloat16 [2, 1024], P(None, 'tensor'), may hold values from -3 to 3
- w_o: bfloat16 [1024, 1024], P('tensor', 'dp'), may hold values from -2 to 2
- w_1: bfloat16 [1024, 4096], P('dp', 'tensor'), may hold values from -0.1875 to 0.1875
- b_1: bfloat16 [4096], P('tensor'), may hold values from -3 to 3
- w_2: bfloat16 [4096, 1024], P('tensor', 'dp'), may hold values from -0.09375 to 0.09375
Outputs:
- block_output: bfloat16 [584, 16, 1024], P('tensor', 'dp')
- grad_inputs: float32 [584, 16, 1024], P('tensor', 'dp')
- grad_ln_gain: float32 [2, 1024], P(None, 'dp')
- grad_d_bias: float32 [4, 1024], P(None, 'dp')
- grad_w_qkv: float32 [1024, 3, 1024], P('dp', None, 'tensor')
- grad_b_qv: float32 [2, 1024], P(None, 'tensor')
- grad_w_o: float32 [1024, 1024], P('tensor', 'dp')
- grad_w_1: float32 [1024, 4096], P('dp', 'tensor')
- grad_b_1: float32 [4096], P('tensor')
- grad_w_2: float32 [4096, 1024], P('tensor', 'dp')
Inputs may be any that keep to these rules, and one draw needn't show every extreme that they name: `valid_mask`: each image has exactly 577 positions marked 1, the others 0.
All inputs are finite; a program needn't handle non-finite values.
Results may differ from a plain program's by a relative error of at most 0.017.
Values may be sent and summed in bfloat16 or wider, within the bound.
A program may use at most 128 MiB of HBM per device.

v0:
```python
import jax
import jax.numpy as jnp
from jax import lax
from jax.sharding import PartitionSpec as P

HD = 64
EPSILON = 1e-06
MASKED = -1e30


def layer_norm(values, gain, shift):
    average = jnp.mean(values, axis=-1, keepdims=True)
    centred = values - average
    variance = jnp.mean(centred * centred, axis=-1, keepdims=True)
    return centred * lax.rsqrt(variance + EPSILON) * gain + shift


def gelu_exact(values):
    return jax.nn.gelu(values, approximate=False)


def gather_layer(ln_gain, d_bias, w_qkv, w_o, w_1, w_2):
    return (
        lax.all_gather(ln_gain, "dp", axis=1, tiled=True),
        lax.all_gather(d_bias, "dp", axis=1, tiled=True),
        lax.all_gather(w_qkv, "dp", axis=0, tiled=True),
        lax.all_gather(w_o, "dp", axis=1, tiled=True),
        lax.all_gather(w_1, "dp", axis=0, tiled=True),
        lax.all_gather(w_2, "dp", axis=1, tiled=True),
    )


def masked_scores(queries, keys_part, valid):
    scores = jnp.einsum(
        "qhd,khd->hqk", queries, keys_part, preferred_element_type=jnp.float32
    ) * HD ** (-0.5)
    return jnp.where(valid[None, None, :] > 0, scores, MASKED)


def attend_forward(bundle):
    packed, valid = bundle
    scores = masked_scores(packed[:, 0], packed[:, 1], valid)
    highest = jnp.max(scores, axis=-1, keepdims=True)
    exponent = jnp.exp(scores - highest)
    denominator = jnp.sum(exponent, axis=-1, keepdims=True)
    attention = (exponent / denominator).astype(jnp.bfloat16)
    mixture = jnp.einsum(
        "hqk,khd->qhd", attention, packed[:, 2], preferred_element_type=jnp.float32
    )
    return (mixture.astype(jnp.bfloat16), (highest + jnp.log(denominator))[..., 0])


def attend_backward(bundle):
    packed, grad_mixture, log_total, valid = bundle
    queries = packed[:, 0]
    keys_part = packed[:, 1]
    values_part = packed[:, 2]
    scores = masked_scores(queries, keys_part, valid)
    attention = jnp.exp(scores - log_total[..., None])
    attention_low = attention.astype(jnp.bfloat16)
    grad_values = jnp.einsum(
        "hqk,qhd->khd", attention_low, grad_mixture, preferred_element_type=jnp.float32
    )
    grad_attention = jnp.einsum(
        "qhd,khd->hqk", grad_mixture, values_part, preferred_element_type=jnp.float32
    )
    inner = jnp.sum(attention * grad_attention, axis=-1, keepdims=True)
    grad_scores = (attention * (grad_attention - inner)).astype(jnp.bfloat16)
    factor = HD ** (-0.5)
    grad_queries = (
        jnp.einsum("hqk,khd->qhd", grad_scores, keys_part, preferred_element_type=jnp.float32)
        * factor
    )
    grad_keys = (
        jnp.einsum("hqk,qhd->khd", grad_scores, queries, preferred_element_type=jnp.float32)
        * factor
    )
    return jnp.stack([grad_queries, grad_keys, grad_values], axis=1)


def body(inputs, valid_mask, cotangent, ln_gain, d_bias, w_qkv, b_qv, w_o, w_1, b_1, w_2):
    local_rows, images, model_width = inputs.shape
    layer = gather_layer(ln_gain, d_bias, w_qkv, w_o, w_1, w_2)
    gains = layer[0].astype(jnp.float32)
    shifts = layer[1].astype(jnp.float32)
    wide_qkv = layer[2].reshape(model_width, -1)
    wide_out = layer[3]
    wide_up = layer[4]
    wide_down = layer[5]
    residual = inputs.astype(jnp.float32)
    normed1 = layer_norm(residual, gains[0], shifts[0]).astype(jnp.bfloat16)
    gathered1 = lax.all_gather(normed1, "tensor", axis=0, tiled=True)
    full_length = gathered1.shape[0]
    columns = b_qv.shape[1]
    heads_local = columns // HD
    projected = jnp.dot(gathered1, wide_qkv, preferred_element_type=jnp.float32).reshape(
        full_length, images, 3, columns
    )
    qkv_bias = jnp.stack([b_qv[0], jnp.zeros_like(b_qv[0]), b_qv[1]]).astype(jnp.float32)
    projected_low = (projected + qkv_bias).astype(jnp.bfloat16)
    per_image = jnp.transpose(projected_low, (1, 0, 2, 3)).reshape(
        images, full_length, 3, heads_local, HD
    )
    mixture, log_total = lax.map(attend_forward, (per_image, valid_mask))
    mixture_seq = jnp.transpose(mixture, (1, 0, 2, 3)).reshape(full_length, images, columns)
    segment = mixture_seq
    attn_sum = lax.psum_scatter(
        jnp.dot(segment, wide_out, preferred_element_type=jnp.float32),
        "tensor",
        scatter_dimension=0,
        tiled=True,
    )
    hidden1 = residual + attn_sum + shifts[2]
    normed2 = layer_norm(hidden1, gains[1], shifts[1]).astype(jnp.bfloat16)
    gathered2 = lax.all_gather(normed2, "tensor", axis=0, tiled=True)
    hidden_in = jnp.dot(gathered2, wide_up, preferred_element_type=jnp.float32) + b_1.astype(
        jnp.float32
    )
    active = gelu_exact(hidden_in).astype(jnp.bfloat16)
    segment = active
    branch_sum = lax.psum_scatter(
        jnp.dot(segment, wide_down, preferred_element_type=jnp.float32).astype(jnp.bfloat16),
        "tensor",
        scatter_dimension=0,
        tiled=True,
    ).astype(jnp.float32)
    block_output = (hidden1 + branch_sum + shifts[3]).astype(jnp.bfloat16)
    layer = gather_layer(ln_gain, d_bias, w_qkv, w_o, w_1, w_2)
    wide_qkv = layer[2].reshape(model_width, -1)
    wide_out = layer[3]
    wide_up = layer[4]
    wide_down = layer[5]
    grad_out = cotangent.astype(jnp.float32)
    grad_gathered = lax.all_gather(cotangent, "tensor", axis=0, tiled=True)
    grad_w_2 = jnp.einsum("sif,sid->fd", active, grad_gathered, preferred_element_type=jnp.float32)
    grad_active = jnp.einsum(
        "sid,fd->sif", grad_gathered, wide_down, preferred_element_type=jnp.float32
    )
    grad_hidden_in = jax.vjp(gelu_exact, hidden_in)[1](grad_active)[0]
    grad_b_1 = jnp.sum(grad_hidden_in, axis=(0, 1))
    grad_hidden_low = grad_hidden_in.astype(jnp.bfloat16)
    grad_w_1 = jnp.einsum(
        "sid,sif->df", gathered2, grad_hidden_low, preferred_element_type=jnp.float32
    )
    segment = grad_hidden_low
    grad_normed2 = lax.psum_scatter(
        jnp.einsum("sif,df->sid", segment, wide_up, preferred_element_type=jnp.float32),
        "tensor",
        scatter_dimension=0,
        tiled=True,
    )
    second_pull = jax.vjp(layer_norm, hidden1, gains[1], shifts[1])[1]
    grad_from_norm, gain2_grad, shift2_grad = second_pull(grad_normed2)
    grad_hidden1 = grad_out + grad_from_norm
    grad_attn_low = grad_hidden1.astype(jnp.bfloat16)
    grad_attn_all = lax.all_gather(grad_attn_low, "tensor", axis=0, tiled=True)
    grad_w_o = jnp.einsum(
        "sic,sid->cd", mixture_seq, grad_attn_all, preferred_element_type=jnp.float32
    )
    grad_mixture = jnp.einsum(
        "sid,cd->sic", grad_attn_all, wide_out, preferred_element_type=jnp.float32
    ).astype(jnp.bfloat16)
    grad_mixture_img = jnp.transpose(
        grad_mixture.reshape(full_length, images, heads_local, HD), (1, 0, 2, 3)
    )
    grad_packed = lax.map(attend_backward, (per_image, grad_mixture_img, log_total, valid_mask))
    grad_projected = jnp.transpose(grad_packed, (1, 0, 2, 3, 4)).reshape(
        full_length, images, 3, columns
    )
    grad_b_qv = jnp.stack(
        [
            jnp.sum(grad_projected[:, :, 0], axis=(0, 1)),
            jnp.sum(grad_projected[:, :, 2], axis=(0, 1)),
        ]
    )
    grad_projected_low = grad_projected.reshape(full_length, images, 3 * columns).astype(
        jnp.bfloat16
    )
    grad_w_qkv = jnp.einsum(
        "sid,sic->dc", gathered1, grad_projected_low, preferred_element_type=jnp.float32
    ).reshape(model_width, 3, columns)
    segment = grad_projected_low
    grad_normed1 = lax.psum_scatter(
        jnp.einsum("sic,dc->sid", segment, wide_qkv, preferred_element_type=jnp.float32).astype(
            jnp.bfloat16
        ),
        "tensor",
        scatter_dimension=0,
        tiled=True,
    ).astype(jnp.float32)
    first_pull = jax.vjp(layer_norm, residual, gains[0], shifts[0])[1]
    grad_from_front, gain1_grad, shift1_grad = first_pull(grad_normed1)
    grad_inputs = grad_hidden1 + grad_from_front
    gain_terms = jnp.stack([gain1_grad, gain2_grad])
    shift_terms = jnp.stack(
        [
            shift1_grad,
            shift2_grad,
            jnp.sum(grad_hidden1, axis=(0, 1)),
            jnp.sum(grad_out, axis=(0, 1)),
        ]
    )
    scattered = (
        lax.psum_scatter(
            gain_terms.astype(jnp.bfloat16), "dp", scatter_dimension=1, tiled=True
        ).astype(jnp.float32),
        lax.psum_scatter(
            shift_terms.astype(jnp.bfloat16), "dp", scatter_dimension=1, tiled=True
        ).astype(jnp.float32),
        lax.psum_scatter(
            grad_w_qkv.astype(jnp.bfloat16), "dp", scatter_dimension=0, tiled=True
        ).astype(jnp.float32),
        lax.psum_scatter(
            grad_w_o.astype(jnp.bfloat16), "dp", scatter_dimension=1, tiled=True
        ).astype(jnp.float32),
        lax.psum_scatter(
            grad_w_1.astype(jnp.bfloat16), "dp", scatter_dimension=0, tiled=True
        ).astype(jnp.float32),
        lax.psum_scatter(
            grad_w_2.astype(jnp.bfloat16), "dp", scatter_dimension=1, tiled=True
        ).astype(jnp.float32),
    )
    gain_sum, shift_sum = lax.psum((scattered[0], scattered[1]), "tensor")
    bias_qv_sum, bias_up_sum = lax.psum((grad_b_qv, grad_b_1), "dp")
    return (
        block_output,
        grad_inputs,
        gain_sum,
        shift_sum,
        scattered[2],
        bias_qv_sum,
        scattered[3],
        scattered[4],
        bias_up_sum,
        scattered[5],
    )


def solution(mesh):
    in_specs = (
        P("tensor", "dp", None),
        P("dp", None),
        P("tensor", "dp", None),
        P(None, "dp"),
        P(None, "dp"),
        P("dp", None, "tensor"),
        P(None, "tensor"),
        P("tensor", "dp"),
        P("dp", "tensor"),
        P("tensor"),
        P("tensor", "dp"),
    )
    out_specs = (
        P("tensor", "dp", None),
        P("tensor", "dp", None),
        P(None, "dp"),
        P(None, "dp"),
        P("dp", None, "tensor"),
        P(None, "tensor"),
        P("tensor", "dp"),
        P("dp", "tensor"),
        P("tensor"),
        P("tensor", "dp"),
    )
    return jax.shard_map(body, mesh=mesh, in_specs=in_specs, out_specs=out_specs, check_vma=False)
```

profile of v0, /device:TPU:0, one launch (start us, length us, event | category | flops | bytes accessed | tf_op | source)
XLA Modules:
  0.0 1150.8 jit_solution(2378708454313699446)
XLA Ops:
  10.7 2.0 fusion.80
  13.0 10.4 all_gather.34
  23.4 8.8 all_gather.35
  32.8 2.9 add_convert_fusion.3
  35.8 10.5 all_gather.38
  46.4 45.4 %all-gather.8.cloned.1.call-done = bf16[584,2,1024]{2,1,0:T(2,128)(2,1)} async-done(((bf16[146,2,1024]{2,1,0:T(2,128)(2,1)}), bf16[584,2,1024]{2,1,0:T(2,128)(2,1)}) %all-gather.8.cloned.1.call-update) | async-done | bytes 2392080 | tf_op jit(solution)/shard_map/all_gather | solution.py:92
  91.8 5.7 fusion.58
  97.4 2.8 copy.121
  100.2 11.2 while.22
  108.8 1.8 fusion.130
  111.5 2.0 fusion.89
  113.5 5.9 copy.123
  120.0 13.1 %all-gather.12.cloned.1.call-start = ((), (), s32[]{:S(2)}) async-start(), calls=%async_computation.8 | async-start | bytes 2990080 | tf_op jit(solution)/shard_map/all_gather | solution.py:115
  134.3 158.0 %all-reduce.11.cloned.1.call-done = f32[584,2,1024]{2,1,0:T(2,128)} async-done(((f32[584,2,1024]{2,1,0:T(2,128)}), f32[584,2,1024]{2,1,0:T(2,128)}) %all-reduce.11.cloned.1.call-update) | async-done | bytes 4784144
  292.3 2.3 fusion.99
  298.8 22.0 %all-gather.14.cloned.1.call-done = bf16[1024,1024]{1,0:T(8,128)(2,1)} async-done(((bf16[128,1024]{1,0:T(8,128)(2,1)}), bf16[1024,1024]{1,0:T(8,128)(2,1)}) %all-gather.14.cloned.1.call-update) | async-done | bytes 2097168 | tf_op jit(solution)/shard_map/all_gather | solution.py:28
  320.8 52.6 %all-gather.12.cloned.1.call-done = bf16[584,2,1024]{2,1,0:T(2,128)(2,1)} async-done(((bf16[146,2,1024]{2,1,0:T(2,128)(2,1)}), bf16[584,2,1024]{2,1,0:T(2,128)(2,1)}) %all-gather.12.cloned.1.call-update) | async-done | bytes 2392080 | tf_op jit(solution)/shard_map/all_gather | solution.py:115
  373.4 6.5 fusion.87
  380.0 2.2 copy-done.8
  382.1 12.1 %multiply_convert_fusion.1 = (bf16[584,2,1024]{2,0,1:T(8,128)(2,1)}, f32[584,2,1024]{2,0,1:T(8,128)}) fusion(f32[584,2,1024]{2,0,1:T(8,128)S(1)} %get-tuple-element.161, f32[1024]{0:T(1024)S(1)} %convert_element_type.124, u8[584,1024]{1,0:T(8,128)(4,1)S(1)} %get-tuple-element.107, u8[584,1024]{1,0:T(8,128)(4,1)S(1)} %get-tuple-element.106), kind=kLoop, calls=%fused_computation.55 | loop fusion | flops 84918272 | bytes 13160448 | tf_op jit(solution)/shard_map/convert_element_type | solution.py:119
  394.2 29.9 %all-gather.18.cloned.1.call-done = bf16[584,2,1024]{2,1,0:T(2,128)(2,1)} async-done(((bf16[146,2,1024]{2,1,0:T(2,128)(2,1)}), bf16[584,2,1024]{2,1,0:T(2,128)(2,1)}) %all-gather.18.cloned.1.call-update) | async-done | bytes 2392080 | tf_op jit(solution)/shard_map/all_gather | solution.py:134
  424.2 28.7 %all-gather.16.cloned.1.call-done = bf16[1024,1024]{1,0:T(8,128)(2,1)} async-done(((bf16[1024,128]{1,0:T(8,128)(2,1)}), bf16[1024,1024]{1,0:T(8,128)(2,1)}) %all-gather.16.cloned.1.call-update) | async-done | bytes 2097168 | tf_op jit(solution)/shard_map/all_gather | solution.py:29
  452.9 9.5 fusion.104
  462.5 2.7 fusion.52
  465.2 5.9 copy.131
  471.1 174.2 %all-reduce.13.cloned.1.call-done = f32[584,2,1024]{2,1,0:T(2,128)} async-done(((f32[584,2,1024]{2,1,0:T(2,128)}), f32[584,2,1024]{2,1,0:T(2,128)}) %all-reduce.13.cloned.1.call-update) | async-done | bytes 4784144
  645.3 3.9 multiply_reduce_fusion.1
  649.5 3.1 fusion.98
  653.6 1.8 fusion.94
  655.5 6.8 bitcast_convert_fusion
  662.3 4.0 copy.172
  666.3 7.1 bitcast_convert_fusion.1
  673.7 31.5 %all-gather.20.cloned.1.call-done = bf16[584,2,1024]{2,1,0:T(2,128)(2,1)} async-done(((bf16[146,2,1024]{2,1,0:T(2,128)(2,1)}), bf16[584,2,1024]{2,1,0:T(2,128)(2,1)}) %all-gather.20.cloned.1.call-update) | async-done | bytes 2392080 | tf_op jit(solution)/shard_map/all_gather | solution.py:156
  705.2 3.7 fusion.72
  708.8 2.1 copy.170
  710.9 3.7 fusion.69
  714.6 2.2 copy.137
  716.7 22.0 %while.23 = (s32[]{:T(128)}, f32[2,584,3,4,64]{1,4,3,2,0:T(8,128)}, bf16[2,584,3,4,64]{1,4,3,2,0:T(8,128)(2,1)S(1)}, s32[2,584]{1,0:T(2,128)S(1)}, f32[2,4,584]{...) while((s32[]{:T(128)}, f32[2,584,3,4,64]{1,4,3,2,0:T(8,128)}, ...), condition=%wide.region_15.16_spmd, body=%wide.region_13.15_spmd.sunk | while | flops 894760960 | bytes 83480296 | solution.py:166
  719.5 2.0 multiply_reduce_fusion.5
  721.6 1.9 multiply_convert_fusion.3
  725.8 1.9 copy-done.2
  730.5 2.0 multiply_reduce_fusion.5
  732.5 1.9 multiply_convert_fusion.3
  736.8 1.9 copy-done.2
  738.8 2.5 bitcast_convert_fusion.2
  741.6 4.0 bitcast_convert_fusion.3
  745.9 5.0 fusion.55
  750.9 4.0 copy.129
  754.9 2.1 convolution_convert_fusion
  757.0 4.0 copy.140
  764.6 27.9 %reduce-scatter.17.cloned.1.call-done = bf16[128,1024]{1,0:T(8,128)(2,1)} async-done(((bf16[1024,1024]{1,0:T(8,128)(2,1)}), bf16[128,1024]{1,0:T(8,128)(2,1)}) %reduce-scatter.17.cloned.1.call-update) | async-done | bytes 262160 | tf_op jit(solution)/shard_map/reduce_scatter | solution.py:216
  792.5 1.8 convert_element_type.144
  794.4 1.9 slice_reduce_fusion.1
  796.3 13.8 %all-reduce.4 = (f32[2,256]{1,0:T(2,128)}, f32[1024]{0:T(1024)}) all-reduce(f32[2,256]{1,0:T(2,128)S(1)} %pad_maximum_fusion.2, f32[1024]{0:T(1024)S(1)} %get-tuple-element.162), channel_id=1, replica_groups=mesh['dp'=8,'tensor'=4] {'dp'}, use_global_device_ids=true, to_apply=%region_32.33 | all-reduce | flops 1536 | bytes 12288 | tf_op jit(solution)/shard_map/psum | solution.py:224
  810.1 19.5 %reduce-scatter.23.cloned.1.call-done = bf16[128,256]{1,0:T(8,128)(2,1)} async-done(((bf16[1024,256]{1,0:T(8,128)(2,1)}), bf16[128,256]{1,0:T(8,128)(2,1)}) %reduce-scatter.23.cloned.1.call-update) | async-done | bytes 65552
  831.3 40.0 %reduce-scatter.15.cloned.1.call-done = bf16[128,3,256]{2,0,1:T(8,128)(2,1)} async-done(((bf16[1024,3,256]{2,0,1:T(8,128)(2,1)}), bf16[128,3,256]{2,0,1:T(8,128)(2,1)}) %reduce-scatter.15.cloned.1.call-update) | async-done | bytes 196624 | tf_op jit(solution)/shard_map/reduce_scatter | solution.py:210
  873.0 174.7 %all-reduce.15.cloned.1.call-done = (bf16[584,2,1024]{2,1,0:T(2,128)(2,1)}, bf16[584,2,1024]{2,1,0:T(2,128)(2,1)}) async-done(((bf16[584,2,1024]{2,1,0:T(2,128)(2,1)}, bf16[584,2,1024]{2,1,0:T(2,128)(2,1)}), (bf16[584,2,1024]{2,1,0:T(2,128)(2,1)}, bf16[584,2,1024]{2,1,0:T(2,128)(2,1)})) %all-reduce.15.cloned.1.call-update) | async-done | bytes 4784144
  1049.3 2.3 fusion.85
  1051.9 4.2 fusion.81
  1056.1 4.5 add_add_fusion.2
  1062.5 2.5 add_convert_fusion.1
  1065.0 29.3 %reduce-scatter.19.cloned.1.call-done = bf16[128,2]{1,0:T(8,128)(2,1)} async-done(((bf16[1024,2]{1,0:T(8,128)(2,1)}), bf16[128,2]{1,0:T(8,128)(2,1)}) %reduce-scatter.19.cloned.1.call-update) | async-done | bytes 528
  1095.1 35.8 %reduce-scatter.21.cloned.1.call-done = bf16[128,4]{1,0:T(8,128)(2,1)} async-done(((bf16[1024,4]{1,0:T(8,128)(2,1)}), bf16[128,4]{1,0:T(8,128)(2,1)}) %reduce-scatter.21.cloned.1.call-update) | async-done | bytes 1040
  1131.8 12.3 %all-reduce.5 = (f32[2,128]{1,0:T(2,128)}, f32[4,128]{1,0:T(4,128)}) all-reduce(bf16[2,128]{1,0:T(2,128)(2,1)S(1)} %copy.167, bf16[4,128]{1,0:T(4,128)(2,1)S(1)} %copy.169), channel_id=1, replica_groups=mesh['dp'=8,'tensor'=4] {'tensor'}, use_global_device_ids=true, to_apply=%region_22.23 | all-reduce | flops 768 | bytes 4608 | tf_op jit(solution)/shard_map/psum | solution.py:223
  (175 shorter events, 43.9 us)
Async XLA Ops:
  7.2 28.6 %copy-start.18 = (bf16[256,128]{1,0:T(8,128)(2,1)S(1)}, bf16[256,128]{1,0:T(8,128)(2,1)}, u32[]{:S(2)}) copy-start(bf16[256,128]{1,0:T(8,128)(2,1)} %param.22) | copy-start | bytes 196612
  7.2 39.1 %copy-start.22 = (bf16[2,256]{1,0:T(2,128)(2,1)S(1)}, bf16[2,256]{1,0:T(2,128)(2,1)}, u32[]{:S(2)}) copy-start(bf16[2,256]{1,0:T(2,128)(2,1)} %param.21) | copy-start | bytes 3076
  7.2 39.2 %all-gather.10.cloned.1.call-start = ((), (), s32[]{:S(2)}) async-start(), calls=%async_computation.7 | async-start | bytes 1769472 | tf_op jit(solution)/shard_map/all_gather | solution.py:26
  9.0 82.7 %all-gather.8.cloned.1.call-start = ((), (), s32[]{:S(2)}) async-start(), calls=%async_computation.6 | async-start | bytes 2990080 | tf_op jit(solution)/shard_map/all_gather | solution.py:92
  10.7 86.8 %copy-start.9 = (f32[146,2]{1,0:T(8,128)}, f32[146,2]{1,0:T(8,128)S(1)}, u32[]{:S(2)}) copy-start(f32[146,2]{1,0:T(8,128)S(1)} %broadcast_multiply_fusion.1) | copy-start | bytes 3508
  12.8 10.5 copy-start.19
  13.0 84.5 %copy-start.11 = (f32[146,2]{1,0:T(8,128)}, f32[146,2]{1,0:T(8,128)S(1)}, u32[]{:S(2)}) copy-start(f32[146,2]{1,0:T(8,128)S(1)} %copy.118) | copy-start | bytes 3508
  32.1 65.3 %copy-start.16 = (f32[1,1024]{1,0:T(1,128)}, f32[1,1024]{1,0:T(1,128)S(1)}, u32[]{:S(2)}) copy-start(f32[1,1024]{1,0:T(1,128)S(1)} %get-tuple-element.158) | copy-start | bytes 12292
  35.7 256.6 %all-reduce.11.cloned.1.call-start = ((), (), s32[]{:S(2)}) async-start(), calls=%async_computation.19 | async-start | bytes 9568256
  97.4 2.8 copy-start.15
  101.8 1.4 copy-start.13
  105.0 0.9 copy-start.14
  107.4 1.4 copy-start.13
  110.6 0.9 copy-start.14
  119.4 13.7 %copy-start.27 = (u32[32]{0:T(128)S(1)}, u32[32]{0:T(128)}, u32[]{:S(2)}) copy-start(u32[32]{0:T(128)} %constant.134) | copy-start | bytes 388
  119.4 201.4 %all-gather.14.cloned.1.call-start = ((), (), s32[]{:S(2)}) async-start(), calls=%async_computation.9 | async-start | bytes 2359296 | tf_op jit(solution)/shard_map/all_gather | solution.py:28
  120.0 253.5 %all-gather.12.cloned.1.call-start = ((), (), s32[]{:S(2)}) async-start(), calls=%async_computation.8 | async-start | bytes 2990080 | tf_op jit(solution)/shard_map/all_gather | solution.py:115
  294.6 4.1 copy-start.23
  297.4 126.8 %all-gather.18.cloned.1.call-start = ((), (), s32[]{:S(2)}) async-start(), calls=%async_computation.11 | async-start | bytes 2990080 | tf_op jit(solution)/shard_map/all_gather | solution.py:134
  298.0 154.9 %all-gather.16.cloned.1.call-start = ((), (), s32[]{:S(2)}) async-start(), calls=%async_computation.10 | async-start | bytes 2359296 | tf_op jit(solution)/shard_map/all_gather | solution.py:29
  298.7 346.6 %all-reduce.13.cloned.1.call-start = ((), (), s32[]{:S(2)}) async-start(), calls=%async_computation.20 | async-start | bytes 9568256
  380.0 2.2 copy-start.8
  452.9 9.6 copy-start.25
  462.4 2.7 copy-start.28
  471.1 234.1 %all-gather.20.cloned.1.call-start = ((), (), s32[]{:S(2)}) async-start(), calls=%async_computation.12 | async-start | bytes 2990080 | tf_op jit(solution)/shard_map/all_gather | solution.py:156
  649.4 4.2 copy-start.5
  652.6 1.0 copy-start.3
  655.5 107.1 %reduce-scatter.25.cloned.1.call-start = ((), (), s32[]{:S(2)}) async-start(), calls=%async_computation.18 | async-start | bytes 2359296
  666.3 126.3 %reduce-scatter.17.cloned.1.call-start = ((), (), s32[]{:S(2)}) async-start(), calls=%async_computation.14 | async-start | bytes 2359296 | tf_op jit(solution)/shard_map/reduce_scatter | solution.py:216
  673.4 156.2 %reduce-scatter.23.cloned.1.call-start = ((), (), s32[]{:S(2)}) async-start(), calls=%async_computation.17 | async-start | bytes 589824
  716.9 1.2 copy-start.7
  723.5 2.1 copy-start.1
  725.8 1.9 copy-start.2
  727.8 1.2 copy-start.7
  734.5 2.2 copy-start.1
  736.8 1.9 copy-start.2
  738.7 132.6 %reduce-scatter.15.cloned.1.call-start = ((), (), s32[]{:S(2)}) async-start(), calls=%async_computation.13 | async-start | bytes 1769472 | tf_op jit(solution)/shard_map/reduce_scatter | solution.py:210
  738.8 2.9 copy-start.24
  745.6 302.1 %all-reduce.15.cloned.1.call-start = ((), (), s32[]{:S(2)}) async-start(), calls=%async_computation.21 | async-start | bytes 9568256
  750.9 4.0 copy-start.26
  760.9 1.1 copy-start.6
  761.0 333.4 %reduce-scatter.19.cloned.1.call-start = ((), (), s32[]{:S(2)}) async-start(), calls=%async_computation.15 | async-start | bytes 294912
  763.8 285.6 %copy-start = (bf16[146,2,1024]{2,1,0:T(2,128)(2,1)S(1)}, bf16[146,2,1024]{2,1,0:T(2,128)(2,1)}, u32[]{:S(2)}) copy-start(bf16[146,2,1024]{2,1,0:T(2,128)(2,1)} %param.15) | copy-start | bytes 1794052
  763.8 285.5 %copy-start.10 = (f32[146,2]{1,0:T(8,128)S(1)}, f32[146,2]{1,0:T(8,128)}, u32[]{:S(2)}) copy-start(f32[146,2]{1,0:T(8,128)} %copy-done.9) | copy-start | bytes 3508
  763.8 285.5 %copy-start.17 = (f32[1,1024]{1,0:T(1,128)S(1)}, f32[1,1024]{1,0:T(1,128)}, u32[]{:S(2)}) copy-start(f32[1,1024]{1,0:T(1,128)} %copy-done.16) | copy-start | bytes 12292
  794.3 257.4 %copy-start.20 = (f32[146,2]{0,1:T(2,128)S(1)}, f32[146,2]{0,1:T(2,128)}, u32[]{:S(2)}) copy-start(f32[146,2]{0,1:T(2,128)} %copy-done.19) | copy-start | bytes 3508
  794.3 257.6 %copy-start.12 = (f32[146,2]{1,0:T(8,128)S(1)}, f32[146,2]{1,0:T(8,128)}, u32[]{:S(2)}) copy-start(f32[146,2]{1,0:T(8,128)} %copy-done.11) | copy-start | bytes 3508
  796.3 259.8 %copy-start.4 = (f32[146,2,1024]{2,1,0:T(2,128)S(1)}, f32[146,2,1024]{2,1,0:T(2,128)}, u32[]{:S(2)}) copy-start(f32[146,2,1024]{2,1,0:T(2,128)} %copy-done.3) | copy-start | bytes 3588100
  1056.1 6.4 copy-start.21
  1061.5 69.4 %reduce-scatter.21.cloned.1.call-start = ((), (), s32[]{:S(2)}) async-start(), calls=%async_computation.16 | async-start | bytes 294912
Sparse Core Ops, SparseCore 0:
  10.5 28.5 all-gather.9
  41.1 50.5 all-gather.7
  119.5 172.7 all-reduce.10
  294.1 26.7 all-gather.13
  322.8 50.5 all-gather.11
  374.9 49.2 all-gather.17
  426.0 26.7 all-gather.15
  471.2 174.0 all-reduce.12
  655.6 49.5 all-gather.19
  708.3 39.7 reduce-scatter.24
  751.4 41.0 reduce-scatter.16
  795.5 34.1 reduce-scatter.22
  832.9 38.3 reduce-scatter.14
  873.6 174.0 all-reduce.14
  1061.7 32.6 reduce-scatter.18
  1097.2 33.7 reduce-scatter.20
where the time goes:
time: 1160 us; the launch traced here: 1150 us
  waiting for transfers between devices  872 us (75%)
  matrix products  77.8 us (7%)
  other arithmetic  64.8 us (6%)
  blocking collectives  55.7 us (5%)
  local copies, waits for them, and re-layouts  51.4 us (4%)
  between operations  15.4 us (1%)
  starting transfers between devices  14.1 us (1%)
    unnamed x23, waiting for transfers between devices  593 us
    all_gather x1, waiting for transfers between devices, body(): gathered2 = lax.all_gather(normed2, 'tensor', axis=0, tiled=True)  52.6 us
    all_gather x1, waiting for transfers between devices, body(): gathered1 = lax.all_gather(normed1, 'tensor', axis=0, tiled=True)  45.4 us
    reduce_scatter x1, waiting for transfers between devices, body(): lax.psum_scatter(grad_w_qkv.astype(jnp.bfloat16), 'dp', scatter_dimension...  40 us
    all_gather x1, waiting for transfers between devices, body(): grad_attn_all = lax.all_gather(grad_attn_low, 'tensor', axis=0, tiled=True)  31.5 us
    all_gather x1, waiting for transfers between devices, body(): grad_gathered = lax.all_gather(cotangent, 'tensor', axis=0, tiled=True)  29.9 us
    all_gather x1, waiting for transfers between devices, gather_layer(): lax.all_gather(w_2, 'dp', axis=1, tiled=True)  28.7 us
    reduce_scatter x1, waiting for transfers between devices, body(): lax.psum_scatter(grad_w_1.astype(jnp.bfloat16), 'dp', scatter_dimension=0...  27.9 us
  transfers between devices with their start and end apart: 16, of which 14 were waited for; matrix products, arithmetic and copies ran while one was open for 10% of the time, Pallas kernels for 0%

commit v1 on v0

--- a/solution.py
+++ b/solution.py
@@ -112,7 +112,23 @@
     )
     hidden1 = residual + attn_sum + shifts[2]
     normed2 = layer_norm(hidden1, gains[1], shifts[1]).astype(jnp.bfloat16)
-    gathered2 = lax.all_gather(normed2, "tensor", axis=0, tiled=True)
+    ways, here, step = (lax.axis_size("tensor"), lax.axis_index("tensor"), normed2.shape[0])
+    shape = [n * ways if d == 0 else n for d, n in enumerate(normed2.shape)]
+    full = lax.dynamic_update_slice_in_dim(
+        jnp.zeros(shape, normed2.dtype), normed2, here * step, axis=0
+    )
+    going_up = going_down = normed2
+    for far in range(1, ways // 2 + 1):
+        going_up = lax.ppermute(going_up, "tensor", [(d, (d + 1) % ways) for d in range(ways)])
+        full = lax.dynamic_update_slice_in_dim(full, going_up, (here - far) % ways * step, axis=0)
+        if 2 * far < ways:
+            going_down = lax.ppermute(
+                going_down, "tensor", [(d, (d - 1) % ways) for d in range(ways)]
+            )
+            full = lax.dynamic_update_slice_in_dim(
+                full, going_down, (here + far) % ways * step, axis=0
+            )
+    gathered2 = full
     hidden_in = jnp.dot(gathered2, wide_up, preferred_element_type=jnp.float32) + b_1.astype(
         jnp.float32
     )

time: 1160 us -> 1110 us (0.957)
  waiting for transfers between devices: 872 us -> 807 us
  local copies, waits for them, and re-layouts: 51.4 us -> 80.9 us
    all_gather x1 -> x0, waiting for transfers between devices: 52.6 us -> none  [body(): gathered2 = lax.all_gather(normed2, 'tensor', axis=0, tiled=True)]
    all_gather x1, waiting for transfers between devices: 29.9 us -> 4.72 us  [body(): grad_gathered = lax.all_gather(cotangent, 'tensor', axis=0, tiled=True)]
    ppermute x0 -> x3, waiting for transfers between devices: none -> 24.2 us  [the longest x2 24.2 us: body(): lax.ppermute(going_up, 'tensor', [(d, (d + 1) % ways) for d in range(ways)])]
    all_gather x1, waiting for transfers between devices: 22 us -> 0.01 us  [gather_layer(): lax.all_gather(w_1, 'dp', axis=0, tiled=True)]
    dynamic_update_slice x0 -> x4, local copies, waits for them, and re-layouts: none -> 18.2 us  [the longest x2 9.09 us: body(): lax.dynamic_update_slice_in_dim(full, going_up, (here - far) % ways * ste...]
    all_gather x1 -> x0, starting transfers between devices: 13.1 us -> none  [body(): gathered2 = lax.all_gather(normed2, 'tensor', axis=0, tiled=True)]
    unnamed x23 -> x22, waiting for transfers between devices: 593 us -> 605 us
  transfers between devices with their start and end apart: 16 -> 18, of which waited for: 14 -> 14; matrix products, arithmetic and copies ran while one was open for 10% -> 13% of each run, Pallas kernels for 0% -> 0%
where the time goes in v1:
time: 1110 us
  waiting for transfers between devices  807 us (73%)
  local copies, waits for them, and re-layouts  80.9 us (7%)
  matrix products  77.3 us (7%)
  other arithmetic  63.8 us (6%)
  blocking collectives  55.5 us (5%)
  between operations  15.4 us (1%)
    unnamed x22, waiting for transfers between devices  605 us
    all_gather x1, waiting for transfers between devices, body(): gathered1 = lax.all_gather(normed1, 'tensor', axis=0, tiled=True)  46.5 us
    reduce_scatter x1, waiting for transfers between devices, body(): lax.psum_scatter(grad_w_qkv.astype(jnp.bfloat16), 'dp', scatter_dimension...  39.9 us
    all_gather x1, waiting for transfers between devices, body(): grad_attn_all = lax.all_gather(grad_attn_low, 'tensor', axis=0, tiled=True)  32 us
    all_gather x1, waiting for transfers between devices, gather_layer(): lax.all_gather(w_2, 'dp', axis=1, tiled=True)  28.1 us
    reduce_scatter x1, waiting for transfers between devices, body(): lax.psum_scatter(grad_w_1.astype(jnp.bfloat16), 'dp', scatter_dimension=0...  26.2 us
    ppermute x2, waiting for transfers between devices, body(): lax.ppermute(going_up, 'tensor', [(d, (d + 1) % ways) for d in range(ways)])  24.2 us
  transfers between devices with their start and end apart: 18, of which 14 were waited for; matrix products, arithmetic and copies ran while one was open for 13% of the time, Pallas kernels for 0%

profile of v1, /device:TPU:0, one launch (start us, length us, event | category | flops | bytes accessed | tf_op | source)
XLA Modules:
  0.0 1105.3 jit_solution(5902295515963264787)
XLA Ops:
  10.8 2.0 fusion.78
  13.0 10.4 all_gather.31
  23.4 8.8 all_gather.32
  34.8 10.4 all_gather.35
  45.3 46.5 %all-gather.7.cloned.1.call-done = bf16[584,2,1024]{2,1,0:T(2,128)(2,1)} async-done(((bf16[146,2,1024]{2,1,0:T(2,128)(2,1)}), bf16[584,2,1024]{2,1,0:T(2,128)(2,1)}) %all-gather.7.cloned.1.call-update) | async-done | bytes 2392080 | tf_op jit(solution)/shard_map/all_gather | solution.py:92
  91.8 5.7 fusion.56
  97.5 2.8 copy.125
  100.2 11.2 %while.22 = (s32[]{:T(128)}, bf16[2,584,4,64]{1,3,2,0:T(8,128)(2,1)}, f32[2,4,584]{2,1,0:T(4,128)S(1)}, bf16[2,584,3,4,64]{1,4,3,2,0:T(8,128)(2,1)S(1)}, s32[2,584]{1,0:T(2,128)S(1)}, /*index=5*/s32[]{:T(128)}) while((s32[]{:T(128)}, bf16[2,584,4,64]{1,3,2,0:T(8,128)(2,1)}, f32[2,4,584]{2,1,0:T(4,128)S(1)}, ...), condition=%wide.region_5.6_spmd, body=%wide.region_2.5_spmd.sunk | while | flops 365759776 | bytes 24867780 | solution.py:104
  111.5 2.0 fusion.87
  113.5 5.9 copy.127
  122.4 170.0 %all-reduce.11.cloned.1.call-done = f32[584,2,1024]{2,1,0:T(2,128)} async-done(((f32[584,2,1024]{2,1,0:T(2,128)}), f32[584,2,1024]{2,1,0:T(2,128)}) %all-reduce.11.cloned.1.call-update) | async-done | bytes 4784144
  292.4 2.3 fusion.97
  297.4 3.8 collective-permute-start.1
  301.2 14.7 %collective-permute-done = bf16[146,2,1024]{2,1,0:T(2,128)(2,1)} collective-permute-done((bf16[146,2,1024]{2,1,0:T(2,128)(2,1)}, bf16[146,2,1024]{2,1,0:T(2,128)(2,1)}, u32[]{:S(2)}, u32[]{:S(2)}) %collective-permute-start) | collective-permute-done | bytes 598048 | tf_op jit(solution)/shard_map/ppermute | solution.py:122
  316.1 2.0 copy.132
  319.8 4.6 dynamic_update_slice.24
  324.4 2.0 copy.133
  326.4 4.5 dynamic_update_slice.25
  331.0 2.1 copy.134
  333.0 4.6 dynamic_update_slice.26
  337.6 9.5 collective-permute-done.2
  347.1 2.0 copy.135
  349.2 4.6 dynamic_update_slice.27
  353.8 6.5 fusion.85
  360.3 2.2 copy-done.9
  362.4 12.2 %multiply_convert_fusion.1 = (bf16[584,2,1024]{2,0,1:T(8,128)(2,1)}, f32[584,2,1024]{2,0,1:T(8,128)}) fusion(f32[584,2,1024]{2,0,1:T(8,128)S(1)} %get-tuple-element.161, f32[1024]{0:T(1024)S(1)} %convert_element_type.124, u8[584,1024]{1,0:T(8,128)(4,1)S(1)} %get-tuple-element.107, u8[584,1024]{1,0:T(8,128)(4,1)S(1)} %get-tuple-element.106), kind=kLoop, calls=%fused_computation.55 | loop fusion | flops 84918272 | bytes 13160448 | tf_op jit(solution)/shard_map/convert_element_type | solution.py:135
  374.7 4.7 all-gather.15.cloned.1.call-done
  379.4 28.1 %all-gather.13.cloned.1.call-done = bf16[1024,1024]{1,0:T(8,128)(2,1)} async-done(((bf16[1024,128]{1,0:T(8,128)(2,1)}), bf16[1024,1024]{1,0:T(8,128)(2,1)}) %all-gather.13.cloned.1.call-update) | async-done | bytes 2097168 | tf_op jit(solution)/shard_map/all_gather | solution.py:29
  407.5 9.5 fusion.102
  417.0 2.7 fusion.49
  419.8 5.9 copy.138
  425.7 174.2 %all-reduce.13.cloned.1.call-done = f32[584,2,1024]{2,1,0:T(2,128)} async-done(((f32[584,2,1024]{2,1,0:T(2,128)}), f32[584,2,1024]{2,1,0:T(2,128)}) %all-reduce.13.cloned.1.call-update) | async-done | bytes 4784144
  599.9 3.7 multiply_reduce_fusion.1
  603.8 3.1 fusion.96
  609.9 6.8 bitcast_convert_fusion
  616.7 4.0 copy.178
  620.7 6.7 bitcast_convert_fusion.1
  627.5 32.0 %all-gather.17.cloned.1.call-done = bf16[584,2,1024]{2,1,0:T(2,128)(2,1)} async-done(((bf16[146,2,1024]{2,1,0:T(2,128)(2,1)}), bf16[584,2,1024]{2,1,0:T(2,128)(2,1)}) %all-gather.17.cloned.1.call-update) | async-done | bytes 2392080 | tf_op jit(solution)/shard_map/all_gather | solution.py:172
  659.5 3.7 fusion.70
  663.2 2.1 copy.176
  665.3 3.6 fusion.67
  668.9 2.2 copy.144
  671.1 23.7 %while.23 = (s32[]{:T(128)}, f32[2,584,3,4,64]{1,4,3,2,0:T(8,128)}, bf16[2,584,3,4,64]{1,4,3,2,0:T(8,128)(2,1)S(1)}, s32[2,584]{1,0:T(2,128)S(1)}, f32[2,4,584]{...) while((s32[]{:T(128)}, f32[2,584,3,4,64]{1,4,3,2,0:T(8,128)}, ...), condition=%wide.region_15.16_spmd, body=%wide.region_13.15_spmd.sunk | while | flops 894760960 | bytes 83480296 | solution.py:182
  674.3 2.0 multiply_reduce_fusion.5
  685.9 2.0 multiply_reduce_fusion.5
  694.9 2.7 bitcast_convert_fusion.2
  697.9 4.0 bitcast_convert_fusion.3
  702.1 5.0 fusion.53
  707.1 4.0 copy.136
  711.1 2.1 convolution_convert_fusion
  713.1 4.0 copy.147
  720.8 26.2 %reduce-scatter.17.cloned.1.call-done = bf16[128,1024]{1,0:T(8,128)(2,1)} async-done(((bf16[1024,1024]{1,0:T(8,128)(2,1)}), bf16[128,1024]{1,0:T(8,128)(2,1)}) %reduce-scatter.17.cloned.1.call-update) | async-done | bytes 262160 | tf_op jit(solution)/shard_map/reduce_scatter | solution.py:232
  748.8 1.9 slice_reduce_fusion.1
  750.8 13.7 %all-reduce.4 = (f32[2,256]{1,0:T(2,128)}, f32[1024]{0:T(1024)}) all-reduce(f32[2,256]{1,0:T(2,128)S(1)} %pad_maximum_fusion.2, f32[1024]{0:T(1024)S(1)} %get-tuple-element.162), channel_id=1, replica_groups=mesh['dp'=8,'tensor'=4] {'dp'}, use_global_device_ids=true, to_apply=%region_32.33 | all-reduce | flops 1536 | bytes 12288 | tf_op jit(solution)/shard_map/psum | solution.py:240
  764.5 19.7 %reduce-scatter.23.cloned.1.call-done = bf16[128,256]{1,0:T(8,128)(2,1)} async-done(((bf16[1024,256]{1,0:T(8,128)(2,1)}), bf16[128,256]{1,0:T(8,128)(2,1)}) %reduce-scatter.23.cloned.1.call-update) | async-done | bytes 65552
  785.8 39.9 %reduce-scatter.15.cloned.1.call-done = bf16[128,3,256]{2,0,1:T(8,128)(2,1)} async-done(((bf16[1024,3,256]{2,0,1:T(8,128)(2,1)}), bf16[128,3,256]{2,0,1:T(8,128)(2,1)}) %reduce-scatter.15.cloned.1.call-update) | async-done | bytes 196624 | tf_op jit(solution)/shard_map/reduce_scatter | solution.py:226
  827.4 174.8 %all-reduce.15.cloned.1.call-done = (bf16[584,2,1024]{2,1,0:T(2,128)(2,1)}, bf16[584,2,1024]{2,1,0:T(2,128)(2,1)}) async-done(((bf16[584,2,1024]{2,1,0:T(2,128)(2,1)}, bf16[584,2,1024]{2,1,0:T(2,128)(2,1)}), (bf16[584,2,1024]{2,1,0:T(2,128)(2,1)}, bf16[584,2,1024]{2,1,0:T(2,128)(2,1)})) %all-reduce.15.cloned.1.call-update) | async-done | bytes 4784144
  1003.9 2.3 fusion.83
  1006.4 4.2 fusion.79
  1010.7 4.5 add_add_fusion.2
  1017.1 2.5 add_convert_fusion.1
  1019.6 29.3 %reduce-scatter.19.cloned.1.call-done = bf16[128,2]{1,0:T(8,128)(2,1)} async-done(((bf16[1024,2]{1,0:T(8,128)(2,1)}), bf16[128,2]{1,0:T(8,128)(2,1)}) %reduce-scatter.19.cloned.1.call-update) | async-done | bytes 528
  1049.7 35.8 %reduce-scatter.21.cloned.1.call-done = bf16[128,4]{1,0:T(8,128)(2,1)} async-done(((bf16[1024,4]{1,0:T(8,128)(2,1)}), bf16[128,4]{1,0:T(8,128)(2,1)}) %reduce-scatter.21.cloned.1.call-update) | async-done | bytes 1040
  1086.3 12.3 %all-reduce.5 = (f32[2,128]{1,0:T(2,128)}, f32[4,128]{1,0:T(4,128)}) all-reduce(bf16[2,128]{1,0:T(2,128)(2,1)S(1)} %copy.173, bf16[4,128]{1,0:T(4,128)(2,1)S(1)} %copy.175), channel_id=1, replica_groups=mesh['dp'=8,'tensor'=4] {'tensor'}, use_global_device_ids=true, to_apply=%region_22.23 | all-reduce | flops 768 | bytes 4608 | tf_op jit(solution)/shard_map/psum | solution.py:239
  (189 shorter events, 61.4 us)
Async XLA Ops:
  7.2 25.6 %copy-start = (bf16[146,2,1024]{2,1,0:T(2,128)(2,1)S(1)}, bf16[146,2,1024]{2,1,0:T(2,128)(2,1)}, u32[]{:S(2)}) copy-start(bf16[146,2,1024]{2,1,0:T(2,128)(2,1)} %param.15) | copy-start | bytes 1794052
  7.2 27.6 %copy-start.19 = (bf16[256,128]{1,0:T(8,128)(2,1)S(1)}, bf16[256,128]{1,0:T(8,128)(2,1)}, u32[]{:S(2)}) copy-start(bf16[256,128]{1,0:T(8,128)(2,1)} %param.22) | copy-start | bytes 196612
  7.2 38.0 %copy-start.23 = (bf16[2,256]{1,0:T(2,128)(2,1)S(1)}, bf16[2,256]{1,0:T(2,128)(2,1)}, u32[]{:S(2)}) copy-start(bf16[2,256]{1,0:T(2,128)(2,1)} %param.21) | copy-start | bytes 3076
  7.2 38.1 %all-gather.9.cloned.1.call-start = ((), (), s32[]{:S(2)}) async-start(), calls=%async_computation.7 | async-start | bytes 1769472 | tf_op jit(solution)/shard_map/all_gather | solution.py:26
  9.1 82.7 %all-gather.7.cloned.1.call-start = ((), (), s32[]{:S(2)}) async-start(), calls=%async_computation.6 | async-start | bytes 2990080 | tf_op jit(solution)/shard_map/all_gather | solution.py:92
  10.7 86.7 %copy-start.10 = (f32[146,2]{1,0:T(8,128)}, f32[146,2]{1,0:T(8,128)S(1)}, u32[]{:S(2)}) copy-start(f32[146,2]{1,0:T(8,128)S(1)} %broadcast_multiply_fusion.1) | copy-start | bytes 3508
  12.9 10.5 copy-start.20
  13.0 84.4 %copy-start.12 = (f32[146,2]{1,0:T(8,128)}, f32[146,2]{1,0:T(8,128)S(1)}, u32[]{:S(2)}) copy-start(f32[146,2]{1,0:T(8,128)S(1)} %copy.122) | copy-start | bytes 3508
  32.2 65.2 %copy-start.17 = (f32[1,1024]{1,0:T(1,128)}, f32[1,1024]{1,0:T(1,128)S(1)}, u32[]{:S(2)}) copy-start(f32[1,1024]{1,0:T(1,128)S(1)} %get-tuple-element.158) | copy-start | bytes 12292
  34.7 257.7 %all-reduce.11.cloned.1.call-start = ((), (), s32[]{:S(2)}) async-start(), calls=%async_computation.18 | async-start | bytes 9568256
  97.4 2.8 copy-start.16
  101.8 1.4 copy-start.14
  105.0 0.9 copy-start.15
  107.4 1.4 copy-start.14
  110.6 0.9 copy-start.15
  119.4 1.8 copy-start.28
  119.4 234.4 %all-gather.11.cloned.1.call-start = ((), (), s32[]{:S(2)}) async-start(), calls=%async_computation.8 | async-start | bytes 2359296 | tf_op jit(solution)/shard_map/all_gather | solution.py:28
  120.0 259.4 %all-gather.15.cloned.1.call-start = ((), (), s32[]{:S(2)}) async-start(), calls=%async_computation.10 | async-start | bytes 2990080 | tf_op jit(solution)/shard_map/all_gather | solution.py:150
  120.6 286.9 %all-gather.13.cloned.1.call-start = ((), (), s32[]{:S(2)}) async-start(), calls=%async_computation.9 | async-start | bytes 2359296 | tf_op jit(solution)/shard_map/all_gather | solution.py:29
  294.7 21.4 %copy-start.24 = (bf16[1024]{0:T(1024)(128)(2,1)S(1)}, bf16[1024]{0:T(1024)(128)(2,1)}, u32[]{:S(2)}) copy-start(bf16[1024]{0:T(1024)(128)(2,1)} %param.24) | copy-start | bytes 6148
  297.4 18.5 %collective-permute-start = (bf16[146,2,1024]{2,1,0:T(2,128)(2,1)}, bf16[146,2,1024]{2,1,0:T(2,128)(2,1)}, u32[]{:S(2)}, u32[]{:S(2)}) collective-permute-start(bf16[146,2,1024]{2,1,0:T(2,128)(2,1)} %add_convert_fusion.2), channel_id=1, source_target_pairs={{0,1},{1,2},{2,3},{3,0},{4,5},{5,6},{6,7},{7,4},{8,9},{9,10},{10,1... | collective-permute-start | bytes 1794056 | tf_op jit(solution)/shard_map/ppermute | solution.py:122
  297.4 33.5 %collective-permute-start.1 = (bf16[146,2,1024]{2,1,0:T(2,128)(2,1)}, bf16[146,2,1024]{2,1,0:T(2,128)(2,1)}, u32[]{:S(2)}, u32[]{:S(2)}) collective-permute-start(bf16[146,2,1024]{2,1,0:T(2,128)(2,1)} %add_convert_fusion.2), channel_id=1, source_target_pairs={{0,3},{1,0},{2,1},{3,2},{4,7},{5,4},{6,5},{7,6},{8,11},{9,8},{10,9... | collective-permute-start | bytes 1794056 | tf_op jit(solution)/shard_map/ppermute | solution.py:125
  315.9 31.2 %collective-permute-start.2 = (bf16[146,2,1024]{2,1,0:T(2,128)(2,1)}, bf16[146,2,1024]{2,1,0:T(2,128)(2,1)}, u32[]{:S(2)}, u32[]{:S(2)}) collective-permute-start(bf16[146,2,1024]{2,1,0:T(2,128)(2,1)} %collective-permute-done), channel_id=1, source_target_pairs={{0,1},{1,2},{2,3},{3,0},{4,5},{5,6},{6,7},{7,4},{8,9},{9,10},{10,1... | collective-permute-start | bytes 1794056 | tf_op jit(solution)/shard_map/ppermute | solution.py:122
  315.9 284.0 %all-reduce.13.cloned.1.call-start = ((), (), s32[]{:S(2)}) async-start(), calls=%async_computation.19 | async-start | bytes 9568256
  360.2 2.2 copy-start.9
  407.5 9.6 copy-start.26
  417.0 2.7 copy-start.29
  425.7 233.9 %all-gather.17.cloned.1.call-start = ((), (), s32[]{:S(2)}) async-start(), calls=%async_computation.11 | async-start | bytes 2990080 | tf_op jit(solution)/shard_map/all_gather | solution.py:172
  603.8 4.2 copy-start.6
  607.0 1.0 copy-start.4
  609.9 108.9 %reduce-scatter.25.cloned.1.call-start = ((), (), s32[]{:S(2)}) async-start(), calls=%async_computation.17 | async-start | bytes 2359296
  620.7 126.3 %reduce-scatter.17.cloned.1.call-start = ((), (), s32[]{:S(2)}) async-start(), calls=%async_computation.13 | async-start | bytes 2359296 | tf_op jit(solution)/shard_map/reduce_scatter | solution.py:232
  627.5 156.7 %reduce-scatter.23.cloned.1.call-start = ((), (), s32[]{:S(2)}) async-start(), calls=%async_computation.16 | async-start | bytes 589824
  671.6 1.2 copy-start.8
  678.9 2.1 copy-start.2
  681.2 1.9 copy-start.3
  683.3 1.2 copy-start.8
  690.5 2.2 copy-start.2
  692.9 1.9 copy-start.3
  694.8 130.9 %reduce-scatter.15.cloned.1.call-start = ((), (), s32[]{:S(2)}) async-start(), calls=%async_computation.12 | async-start | bytes 1769472 | tf_op jit(solution)/shard_map/reduce_scatter | solution.py:226
  694.8 3.0 copy-start.25
  701.9 300.4 %all-reduce.15.cloned.1.call-start = ((), (), s32[]{:S(2)}) async-start(), calls=%async_computation.20 | async-start | bytes 9568256
  707.1 4.0 copy-start.27
  717.1 1.1 copy-start.7
  717.2 331.7 %reduce-scatter.19.cloned.1.call-start = ((), (), s32[]{:S(2)}) async-start(), calls=%async_computation.14 | async-start | bytes 294912
  720.8 283.1 %copy-start.1 = (bf16[146,2,1024]{2,1,0:T(2,128)(2,1)S(1)}, bf16[146,2,1024]{2,1,0:T(2,128)(2,1)}, u32[]{:S(2)}) copy-start(bf16[146,2,1024]{2,1,0:T(2,128)(2,1)} %param.15) | copy-start | bytes 1794052
  720.8 283.1 %copy-start.11 = (f32[146,2]{1,0:T(8,128)S(1)}, f32[146,2]{1,0:T(8,128)}, u32[]{:S(2)}) copy-start(f32[146,2]{1,0:T(8,128)} %copy-done.10) | copy-start | bytes 3508
  720.8 283.1 %copy-start.18 = (f32[1,1024]{1,0:T(1,128)S(1)}, f32[1,1024]{1,0:T(1,128)}, u32[]{:S(2)}) copy-start(f32[1,1024]{1,0:T(1,128)} %copy-done.17) | copy-start | bytes 12292
  748.8 257.5 %copy-start.21 = (f32[146,2]{0,1:T(2,128)S(1)}, f32[146,2]{0,1:T(2,128)}, u32[]{:S(2)}) copy-start(f32[146,2]{0,1:T(2,128)} %copy-done.20) | copy-start | bytes 3508
  748.8 257.6 %copy-start.13 = (f32[146,2]{1,0:T(8,128)S(1)}, f32[146,2]{1,0:T(8,128)}, u32[]{:S(2)}) copy-start(f32[146,2]{1,0:T(8,128)} %copy-done.12) | copy-start | bytes 3508
  750.8 259.9 %copy-start.5 = (f32[146,2,1024]{2,1,0:T(2,128)S(1)}, f32[146,2,1024]{2,1,0:T(2,128)}, u32[]{:S(2)}) copy-start(f32[146,2,1024]{2,1,0:T(2,128)} %copy-done.4) | copy-start | bytes 3588100
  1010.7 6.4 copy-start.22
  1016.1 69.4 %reduce-scatter.21.cloned.1.call-start = ((), (), s32[]{:S(2)}) async-start(), calls=%async_computation.15 | async-start | bytes 294912
Sparse Core Ops, SparseCore 0:
  10.5 28.4 all-gather.8
  41.1 50.5 all-gather.6
  119.5 172.7 all-reduce.10
  294.1 26.7 all-gather.10
  322.3 57.0 all-gather.14
  381.1 26.2 all-gather.12
  425.8 174.0 all-reduce.12
  610.0 49.5 all-gather.16
  662.8 39.7 reduce-scatter.24
  705.8 41.1 reduce-scatter.16
  750.0 34.0 reduce-scatter.22
  787.3 38.3 reduce-scatter.14
  828.1 174.0 all-reduce.14
  1016.2 32.6 reduce-scatter.18
  1051.7 33.7 reduce-scatter.20
